TPU v7x, 1024 devices: a whole 4x4x32 slice. The times are simulated.
1024 devices in a mesh: dp: 8 (over x, core), expert: 128 (over z, y).
Axes of the slice: x: 4, y: 4, z: 32, core: 2. Of those that a mesh axis runs over, the one named last changes fastest.
Arguments:
- tokens: bfloat16 [512, 7168], P('dp', 'expert'), parts along dimension 0, may hold values from -6 to 6
- routes: int32 [512, 8], P('dp'), parts along dimension 0, may hold values from 0 to 15, all different within a row; in each aligned block of 64 rows (0 to 63, 64 to 127, ...) at most 40 rows name the same one
- gate_values: bfloat16 [512, 8], P('dp'), parts along dimension 0, may hold values from 0.049804688 to 1
- gate_weight: bfloat16 [7168, 16384], P(None, 'expert'), may hold values from -0.0625 to 0.0625
- up_weight: bfloat16 [7168, 16384], P(None, 'expert'), may hold values from -0.0625 to 0.0625
- down_weight: bfloat16 [16384, 7168], P(None, 'expert'), may hold values from -0.1875 to 0.1875
Outputs:
- layer_output: bfloat16 [512, 7168], P('dp', 'expert'), parts along dimension 0
There are 8 independent parts, one for each index of `dp`. A program takes and returns all parts, laid end to end along the dimension named above; an argument that names none is the same for every part. Nothing has to cross between parts.
Inputs may be any that keep to these rules, and one draw needn't show every extreme that they name: `routes`: each row names 8 different experts; no expert is named by more than 40 rows of a group, a bound that some block reaches.
All inputs are finite; a program needn't handle non-finite values.
Results may differ from a plain program's by a relative error of at most 0.0049.
Values may be sent and summed in bfloat16 or wider, within the bound.
No kernel may reach another device: no remote copies, remote signals or barrier semaphores. Data moves between devices by JAX's collectives and lax.ppermute only.
A program may use at most 32 MiB of HBM per device.

v0:
```python
import jax
import jax.numpy as jnp
from jax import lax
from jax.sharding import Mesh
from jax.sharding import PartitionSpec as P

HIDDEN_SIZE = 1024
EXPERTS = 16
EXPERT = ("expert_0", "expert_1")


def laid_out(pieces, dim):
    lengths = list(pieces.shape[1:])
    lengths[dim] *= pieces.shape[0]
    return jnp.moveaxis(pieces, 0, dim).reshape(lengths)


def stacked_from(x, axes, turns):
    pieces = x
    for k in turns:
        pieces = lax.all_gather(pieces, axes[k])
    done = turns[::-1]
    back = [done.index(k) for k in range(len(axes))]
    pieces = pieces.transpose(*back, *range(len(axes), pieces.ndim))
    return pieces.reshape(-1, *x.shape)


def whole_of(x, axes, turns, dim):
    return laid_out(stacked_from(x, axes, turns), dim)


def body(tokens, routes, gate_values, gate_weight, up_weight, down_weight):
    unit_count = gate_weight.shape[1]
    span_units = min(unit_count, HIDDEN_SIZE)
    local_count = unit_count // span_units
    token_count = tokens.shape[0]
    first_expert = lax.axis_index(EXPERT) * unit_count // HIDDEN_SIZE
    matched = routes[:, :, None] == lax.broadcasted_iota(jnp.int32, (1, 1, EXPERTS), 2)
    combine_table = jnp.sum(
        jnp.where(matched, gate_values[:, :, None].astype(jnp.float32), 0.0), axis=1
    )
    selector = (
        lax.broadcasted_iota(jnp.int32, (EXPERTS, local_count), 0)
        == first_expert + lax.broadcasted_iota(jnp.int32, (EXPERTS, local_count), 1)
    ).astype(jnp.float32)
    local_gates = jnp.dot(
        combine_table, selector, precision=lax.Precision.HIGHEST, preferred_element_type=jnp.float32
    )
    all_rows = whole_of(tokens, EXPERT, (0, 1), 1)
    empty = jnp.zeros((token_count, down_weight.shape[1]), jnp.float32)
    capacity = token_count * routes.shape[1] * 5 // (EXPERTS * 4)
    present = combine_table > 0.0
    slot = jnp.cumsum(present.astype(jnp.int32), axis=0) - 1
    placement = jnp.logical_and(
        present[:, :, None],
        slot[:, :, None] == lax.broadcasted_iota(jnp.int32, (1, 1, capacity), 2),
    )
    placement = placement.astype(jnp.bfloat16)
    place = lax.dynamic_slice_in_dim(placement, first_expert + 0, 1, 1)[:, 0, :]
    picked = jnp.dot(place.T, all_rows, preferred_element_type=jnp.float32).astype(jnp.bfloat16)
    weights = jnp.dot(
        place.T.astype(jnp.float32),
        local_gates,
        precision=lax.Precision.HIGHEST,
        preferred_element_type=jnp.float32,
    )
    low = 0
    gate_proj = jnp.dot(picked, gate_weight, preferred_element_type=jnp.float32)
    up_proj = jnp.dot(picked, up_weight, preferred_element_type=jnp.float32)
    pieces = (jax.nn.silu(gate_proj) * up_proj * weights).astype(jnp.bfloat16)
    gathered = whole_of(pieces, EXPERT, (0, 1), 1)
    result = empty
    for expert in range(EXPERTS):
        low = expert * HIDDEN_SIZE
        outputs = jnp.dot(
            gathered[:, low : low + HIDDEN_SIZE],
            down_weight[low : low + HIDDEN_SIZE, :],
            preferred_element_type=jnp.float32,
        )
        result = result + jnp.dot(
            placement[:, expert, :].astype(jnp.float32),
            outputs,
            precision=lax.Precision.HIGHEST,
            preferred_element_type=jnp.float32,
        )
    return result.astype(jnp.bfloat16)


def solution(mesh):
    split = Mesh(mesh.devices.reshape(mesh.shape["dp"], 32, 4), ("dp", "expert_0", "expert_1"))
    return jax.shard_map(
        body,
        mesh=split,
        in_specs=(
            P("dp", EXPERT),
            P("dp", None),
            P("dp", None),
            P(None, EXPERT),
            P(None, EXPERT),
            P(None, EXPERT),
        ),
        out_specs=P("dp", EXPERT),
        check_vma=False,
    )
```

profile of v0, /device:TPU:6, one launch (start us, length us, event | category | flops | bytes accessed | tf_op | source)
XLA Modules:
  0.0 209.3 jit_solution(5009040674535423717)
XLA Ops:
  6.5 0.0 copy-start
  6.5 0.0 all-gather.7.cloned.1.call-start
  6.5 0.8 convert_element_type.15
  7.4 0.7 select_reduce_fusion
  8.1 0.1 convolution_bitcast_fusion
  8.2 70.6 %all-gather.4 = bf16[32,64,56]{1,2,0:T(8,128)(2,1)S(1)} all-gather(bf16[1,64,56]{1,2,0:T(8,128)(2,1)} %bitcast.124), channel_id=2, replica_groups=mesh['dp'=8,'expert_0'=32,'expert_1'=4] {'expert_0'}, dimensions={0}, use_global_device_ids=true | all-gather | bytes 236544 | tf_op jit(solution)/shard_map/all_gather | solution.py:21
  78.8 15.9 %all-gather.1 = bf16[128,64,56]{1,2,0:T(8,128)(2,1)S(1)} all-gather(bf16[32,64,56]{1,2,0:T(8,128)(2,1)S(1)} %all-gather.4), channel_id=3, replica_groups=mesh['dp'=8,'expert_0'=32,'expert_1'=4] {'expert_1'}, dimensions={0}, use_global_device_ids=true | all-gather | bytes 1146880 | tf_op jit(solution)/shard_map/all_gather | solution.py:21
  94.7 1.4 copy.34
  96.2 0.1 copy.32
  96.3 0.1 reduce_window_sum.11
  96.4 0.1 copy.33
  96.4 0.1 fusion.3
  96.5 0.0 copy-start.1
  96.5 2.3 %convolution_convert_fusion = bf16[40,7168]{1,0:T(8,128)(2,1)S(1)} fusion(bf16[64,7168]{0,1:T(8,128)(2,1)} %bitcast.103, pred[64,16,40]{0,2,1:T(8,128)(4,1)S(1)} %fusion.3, s32[]{:T(128)S(6)} %select_n.14), kind=kOutput, calls=%fused_computation | convolution fusion | flops 36986880 | bytes 1496068 | tf_op jit(solution)/shard_map/dot_general | solution.py:60
  98.9 0.1 convolution_bitcast_fusion.1
  99.0 0.0 copy-done
  99.0 0.5 fusion.60
  99.5 0.0 copy-done.1
  99.5 0.4 fusion.2
  99.9 57.8 %all-gather.2 = bf16[1280,128]{1,0:T(8,128)(2,1)} all-gather(bf16[40,128]{1,0:T(8,128)(2,1)S(1)} %fusion.2), channel_id=4, replica_groups=mesh['dp'=8,'expert_0'=32,'expert_1'=4] {'expert_0'}, dimensions={0}, use_global_device_ids=true | all-gather | bytes 337920 | tf_op jit(solution)/shard_map/all_gather | solution.py:21
  157.7 0.0 all-gather.7.cloned.1.call-update
  157.7 34.8 %all-gather.7.cloned.1.call-done = bf16[128,40,128]{2,1,0:T(8,128)(2,1)} async-done(((bf16[32,40,128]{2,1,0:T(8,128)(2,1)}), bf16[128,40,128]{2,1,0:T(8,128)(2,1)}) %all-gather.7.cloned.1.call-update) | async-done | bytes 1310736 | tf_op jit(solution)/shard_map/all_gather | solution.py:21
  192.6 1.4 copy.36
  194.0 0.0 copy-start.2
  194.0 0.2 copy.41
  194.2 1.3 copy-done.2
  195.5 0.1 fusion.34
  195.6 0.2 fusion.32
  195.8 0.2 fusion.30
  196.0 0.2 fusion.28
  196.1 0.2 fusion.26
  196.3 0.2 fusion.24
  196.5 0.2 fusion.22
  196.6 0.2 fusion.20
  196.8 0.2 fusion.18
  197.0 0.2 fusion.16
  197.1 0.2 fusion.14
  197.3 0.2 fusion.12
  197.5 0.2 fusion.10
  197.6 0.2 fusion.8
  197.8 0.2 fusion.6
  198.0 0.2 fusion.4
  198.1 0.2 fusion.52
  198.4 0.2 convolution_add_fusion.14
  198.6 0.2 convolution_add_fusion.13
  198.8 0.2 convolution_add_fusion.12
  199.1 0.2 convolution_add_fusion.11
  199.3 0.2 convolution_add_fusion.10
  199.5 0.2 convolution_add_fusion.9
  199.8 0.2 convolution_add_fusion.8
  200.0 0.2 convolution_add_fusion.7
  200.2 0.2 convolution_add_fusion.6
  200.4 0.2 convolution_add_fusion.5
  200.7 0.2 convolution_add_fusion.4
  200.9 0.2 convolution_add_fusion.3
  201.1 0.2 convolution_add_fusion.2
  201.4 0.2 convolution_add_fusion.1
  201.6 0.8 fusion
  (2 shorter events, 0.0 us)
Async XLA Ops:
  6.5 92.5 %copy-start = (bf16[7168,128]{1,0:T(8,128)(2,1)S(1)}, bf16[7168,128]{1,0:T(8,128)(2,1)}, u32[]{:S(2)}) copy-start(bf16[7168,128]{1,0:T(8,128)(2,1)} %param.9) | copy-start | bytes 5505028
  6.5 186.0 %all-gather.7.cloned.1.call-start = ((), (), s32[]{:S(2)}) async-start(), calls=%async_computation | async-start | bytes 1638400 | tf_op jit(solution)/shard_map/all_gather | solution.py:21
  96.5 3.0 %copy-start.1 = (bf16[7168,128]{1,0:T(8,128)(2,1)S(1)}, bf16[7168,128]{1,0:T(8,128)(2,1)}, u32[]{:S(2)}) copy-start(bf16[7168,128]{1,0:T(8,128)(2,1)} %param.10) | copy-start | bytes 5505028
  194.0 1.5 copy-start.2
Sparse Core Ops, SparseCore 0:
  157.8 34.6 all-gather.6
where the time goes:
time: 210 us; the launch traced here: 209 us
  blocking collectives  144 us (69%)
  waiting for transfers between devices  34.8 us (17%)
  between operations  13.6 us (6%)
  matrix products  10.3 us (5%)
  local copies, waits for them, and re-layouts  4.49 us (2%)
    all_gather x3, blocking collectives, stacked_from(): pieces = lax.all_gather(pieces, axes[k])  144 us
    all_gather x1, waiting for transfers between devices, stacked_from(): pieces = lax.all_gather(pieces, axes[k])  34.8 us
    dot_general x16, matrix products, body(): jnp.dot(placement[:, expert, :].astype(jnp.float32), outputs, precision=l...  4.2 us
  transfers between devices with their start and end apart: 1, of which 1 were waited for; matrix products, arithmetic and copies ran while one was open for 0% of the time, Pallas kernels for 0%

commit v1 on v0

v1 whole, which is shorter than its diff:
```python
import jax
import jax.numpy as jnp
from jax import lax
from jax.sharding import Mesh
from jax.sharding import PartitionSpec as P

HIDDEN_SIZE = 1024
EXPERTS = 16
GROUP = ("expert_0", "expert_1", "expert_2")
NEAR = ("expert_1", "expert_2")


def spread(x):
    far = lax.all_gather(x[None], "expert_0", tiled=True)
    near = jnp.broadcast_to(far[None], (8, *far.shape))
    return lax.all_to_all(near, NEAR, 0, 0)


def body(tokens, routes, gate_values, gate_weight, up_weight, down_weight):
    token_count = tokens.shape[0]
    expert = lax.axis_index("expert_0")
    matched = routes[:, :, None] == lax.broadcasted_iota(jnp.int32, (1, 1, EXPERTS), 2)
    combine_table = jnp.sum(
        jnp.where(matched, gate_values[:, :, None].astype(jnp.float32), 0.0), axis=1
    )
    weights = lax.dynamic_slice_in_dim(combine_table, expert, 1, 1)
    capacity = token_count * routes.shape[1] * 5 // (EXPERTS * 4)
    present = combine_table > 0.0
    slot = jnp.cumsum(present.astype(jnp.int32), axis=0) - 1
    placement = jnp.logical_and(
        present[:, :, None],
        slot[:, :, None] == lax.broadcasted_iota(jnp.int32, (1, 1, capacity), 2),
    ).astype(jnp.bfloat16)
    place = lax.dynamic_slice_in_dim(placement, expert, 1, 1)[:, 0, :]

    columns = tokens.T
    packed = jnp.concatenate([columns[:32], jnp.pad(columns[32:], ((0, 8), (0, 0)))], axis=1)
    parts = spread(packed).transpose(1, 0, 2, 3)
    features = jnp.concatenate([parts[..., :64], parts[:, :, :24, 64:]], axis=2)
    features = features.reshape(-1, token_count)
    dims = (((0,), (0,)), ((), ()))
    gate_proj = lax.dot_general(features, gate_weight, dims, preferred_element_type=jnp.float32)
    up_proj = lax.dot_general(features, up_weight, dims, preferred_element_type=jnp.float32)
    hidden = (jax.nn.silu(gate_proj) * up_proj * weights).astype(jnp.bfloat16)
    pieces = lax.dot_general(place, hidden, dims, preferred_element_type=jnp.float32)
    gathered = spread(pieces.astype(jnp.bfloat16))
    full = lax.dot_general(
        placement, gathered, (((2,), (2,)), ((1,), (1,))), preferred_element_type=jnp.float32
    ).astype(jnp.bfloat16)
    full = full.transpose(1, 0, 2, 3).reshape(token_count, -1)
    result = jnp.dot(full, down_weight, preferred_element_type=jnp.float32)
    return result.astype(jnp.bfloat16)


def solution(mesh):
    split = Mesh(
        mesh.devices.reshape(mesh.shape["dp"], 16, 2, 4),
        ("dp", *GROUP),
    )
    return jax.shard_map(
        body,
        mesh=split,
        in_specs=(
            P("dp", GROUP),
            P("dp", None),
            P("dp", None),
            P(None, GROUP),
            P(None, GROUP),
            P(None, GROUP),
        ),
        out_specs=P("dp", GROUP),
        check_vma=False,
    )
```

time: 210 us -> 133 us (0.63)
  blocking collectives: 144 us -> 95.9 us
  waiting for transfers between devices: 34.8 us -> 10.2 us
  between operations: 13.6 us -> 0.11 us
  local copies, waits for them, and re-layouts: 4.49 us -> 13.2 us
  starting transfers between devices: 0.01 us -> 4.84 us
  matrix products: 10.3 us -> 6.03 us
    all_gather x3 -> x2, blocking collectives: 144 us -> 79.7 us  [spread(): far = lax.all_gather(x[None], 'expert_0', tiled=True)]
    all_gather x1 -> x0, waiting for transfers between devices: 34.8 us -> none  [stacked_from(): pieces = lax.all_gather(pieces, axes[k])]
    all_to_all x0 -> x1, blocking collectives: none -> 16.2 us  [spread(): return lax.all_to_all(near, NEAR, 0, 0)]
    all_to_all x0 -> x1, waiting for transfers between devices: none -> 10.2 us  [spread(): return lax.all_to_all(near, NEAR, 0, 0)]
    all_to_all x0 -> x1, starting transfers between devices: none -> 4.84 us  [spread(): return lax.all_to_all(near, NEAR, 0, 0)]
    concatenate x0 -> x1, local copies, waits for them, and re-layouts: none -> 4.42 us  [body(): features = jnp.concatenate([parts[..., :64], parts[:, :, :24, 64:]], axis=2)]
    dot_general x37 -> x4, matrix products: 10.3 us -> 6.03 us  [the longest x1 2.75 us: body(): result = jnp.dot(full, down_weight, preferred_element_type=jnp.float32)]
    reshape x1, local copies, waits for them, and re-layouts: 0.23 us -> 3.98 us  [body(): features = features.reshape(-1, token_count)]
where the time goes in v1:
time: 133 us; the launch traced here: 132 us
  blocking collectives  95.9 us (72%)
  local copies, waits for them, and re-layouts  13.2 us (10%)
  waiting for transfers between devices  10.2 us (8%)
  matrix products  6.03 us (5%)
  starting transfers between devices  4.84 us (4%)
  other arithmetic  1.88 us (1%)
    all_gather x2, blocking collectives, spread(): far = lax.all_gather(x[None], 'expert_0', tiled=True)  79.7 us
    all_to_all x1, blocking collectives, spread(): return lax.all_to_all(near, NEAR, 0, 0)  16.2 us
    all_to_all x1, waiting for transfers between devices, spread(): return lax.all_to_all(near, NEAR, 0, 0)  10.2 us
    all_to_all x1, starting transfers between devices, spread(): return lax.all_to_all(near, NEAR, 0, 0)  4.84 us
    concatenate x1, local copies, waits for them, and re-layouts, body(): features = jnp.concatenate([parts[..., :64], parts[:, :, :24, 64:]], axis=2)  4.42 us
    reshape x1, local copies, waits for them, and re-layouts, body(): features = features.reshape(-1, token_count)  3.98 us
    dot_general x1, matrix products, body(): result = jnp.dot(full, down_weight, preferred_element_type=jnp.float32)  2.75 us
  transfers between devices with their start and end apart: 1, of which 1 were waited for; matrix products, arithmetic and copies ran while one was open for 0% of the time, Pallas kernels for 0%

profile of v1, /device:TPU:6, one launch (start us, length us, event | category | flops | bytes accessed | tf_op | source)
XLA Modules:
  0.0 132.1 jit_solution(16830028762955682759)
XLA Ops:
  0.0 0.0 copy-start
  0.0 0.0 copy-start.2
  0.0 0.0 copy-start.1
  0.0 0.8 slice.17
  0.8 0.7 slice.16
  1.5 0.1 fusion.23
  1.6 47.5 %all-gather = bf16[512,128]{1,0:T(8,128)(2,1)S(1)} all-gather(bf16[32,128]{1,0:T(8,128)(2,1)S(1)} %fusion.23), channel_id=2, replica_groups=mesh['dp'=8,'expert_0'=16,'expert_1'=2,'expert_2'=4] {'expert_0'}, dimensions={0}, use_global_device_ids=true | all-gather | bytes 139264 | tf_op jit(solution)/shard_map/all_gather | solution.py:14
  49.1 1.2 broadcast_in_dim.37
  50.2 4.8 %all-to-all-start = ((bf16[8,16,32,128]{3,2,1,0:T(8,128)(2,1)}), bf16[8,16,32,128]{3,2,1,0:T(8,128)(2,1)S(1)}, u32[]{:S(2)}, u32[]{:S(2)}) async-start(bf16[8,16,32,128]{3,2,1,0:T(8,128)(2,1)} %broadcast_in_dim.37), calls=%async_computation | async-start | bytes 2097152 | tf_op jit(solution)/shard_map/all_to_all | solution.py:16
  55.1 0.0 copy-done.2
  55.1 0.0 copy-done.1
  55.2 0.1 copy.24
  55.2 0.1 reduce_window_sum.11
  55.3 0.1 copy.25
  55.4 0.1 fusion.11
  55.5 10.2 %all-to-all-done = bf16[8,16,32,128]{3,2,1,0:T(8,128)(2,1)S(1)} async-done(((bf16[8,16,32,128]{3,2,1,0:T(8,128)(2,1)}), bf16[8,16,32,128]{3,2,1,0:T(8,128)(2,1)S(1)}, u32[]{:S(2)}, u32[]{:S(2)}) %all-to-all-start) | async-done | bytes 1048608 | tf_op jit(solution)/shard_map/all_to_all | solution.py:16
  65.7 0.3 slice.19
  66.0 1.6 %pad_maximum_fusion = bf16[16,8,56,64]{3,2,0,1:T(8,128)(2,1)} fusion(bf16[16,8,24,64]{3,2,0,1:T(8,128)(2,1)S(1)} %slice.19, bf16[16,8,32,64]{3,2,0,1:T(8,128)(2,1)S(1)} %bitcast.34), kind=kLoop, calls=%fused_computation.4 | loop fusion | flops 1835008 | bytes 1835008 | tf_op jit(solution)/shard_map/concatenate | solution.py:39
  67.6 4.4 %copy.26 = bf16[16,8,56,64]{2,1,0,3:T(8,128)(2,1)} copy(bf16[16,8,56,64]{3,2,0,1:T(8,128)(2,1)} %pad_maximum_fusion) | data formatting | bytes 1835008 | tf_op jit(solution)/shard_map/concatenate | solution.py:39
  72.0 4.0 %reshape.24 = bf16[7168,64]{0,1:T(8,128)(2,1)S(1)} reshape(bf16[16,8,56,64]{2,1,0,3:T(8,128)(2,1)} %copy.26) | data formatting | bytes 1835008 | tf_op jit(solution)/shard_map/reshape | solution.py:40
  76.0 0.0 copy-done
  76.0 0.5 fusion.28
  76.4 2.1 %fusion.10 = bf16[40,128]{1,0:T(8,128)(2,1)S(1)} fusion(bf16[7168,64]{0,1:T(8,128)(2,1)S(1)} %reshape.24, bf16[7168,128]{1,0:T(8,128)(2,1)} %param.10, f32[64,128]{1,0:T(8,128)S(1)} %fusion.28, pred[64,16,40]{0,2,1:T(8,128)(4,1)S(1)} %fusion.11, s32[]{:T(128)S(6)} %select_n.9, f32[64]{0:T(128)S(1)} %dynamic-slice_bitcast_fusion), kind=kOutput, calls=%fused_computation.11 | convolution fusion | flops 118158336 | bytes 2801156 | tf_op jit(solution)/shard_map/dot_general | solution.py:45
  78.5 32.3 %all-gather.1 = bf16[640,128]{1,0:T(8,128)(2,1)S(1)} all-gather(bf16[40,128]{1,0:T(8,128)(2,1)S(1)} %fusion.10), channel_id=3, replica_groups=mesh['dp'=8,'expert_0'=16,'expert_1'=2,'expert_2'=4] {'expert_0'}, dimensions={0}, use_global_device_ids=true | all-gather | bytes 174080 | tf_op jit(solution)/shard_map/all_gather | solution.py:14
  110.8 0.2 broadcast_in_dim.39
  111.0 16.2 %all_to_all.10 = bf16[8,16,40,128]{3,2,1,0:T(8,128)(2,1)S(1)} all-to-all(bf16[8,16,40,128]{3,2,1,0:T(8,128)(2,1)S(1)} %broadcast_in_dim.39), channel_id=1, replica_groups=mesh['dp'=8,'expert_0'=16,'expert_1'=2,'expert_2'=4] {'expert_1','expert..., dimensions={0} | all-to-all | bytes 2621440 | tf_op jit(solution)/shard_map/all_to_all | solution.py:16
  127.1 0.8 convert_bitcast_fusion
  127.9 0.0 copy-start.3
  127.9 1.4 %copy.28 = bf16[64,16,8,128]{3,2,1,0:T(8,128)(2,1)S(1)} copy(bf16[64,16,8,128]{3,0,2,1:T(8,128)(2,1)S(1)} %convert_bitcast_fusion) | data formatting | bytes 4194304 | tf_op jit(solution)/shard_map/convert_element_type | solution.py:49
  129.3 0.1 copy-done.3
  129.4 2.7 %fusion.6 = bf16[64,56]{0,1:T(8,128)(2,1)} fusion(bf16[16384,56]{0,1:T(8,128)(2,1)S(1)} %copy-done.3, bf16[8,8,128,128]{3,2,1,0:T(8,128)(2,1)S(1)} %bitcast.35), kind=kOutput, calls=%fused_computation.9 | convolution fusion | flops 117444096 | bytes 3939328 | tf_op jit(solution)/shard_map/dot_general | solution.py:51
  (5 shorter events, 0.0 us)
Async XLA Ops:
  0.0 76.0 %copy-start = (bf16[7168,128]{1,0:T(8,128)(2,1)S(1)}, bf16[7168,128]{1,0:T(8,128)(2,1)}, u32[]{:S(2)}) copy-start(bf16[7168,128]{1,0:T(8,128)(2,1)} %param.9) | copy-start | bytes 5505028
  0.0 55.1 %copy-start.2 = (bf16[64,8]{0,1:T(8,128)(2,1)S(1)}, bf16[64,8]{0,1:T(8,128)(2,1)}, u32[]{:S(2)}) copy-start(bf16[64,8]{0,1:T(8,128)(2,1)} %param.8) | copy-start | bytes 3076
  0.0 55.1 %copy-start.1 = (s32[64,8]{0,1:T(8,128)S(1)}, s32[64,8]{0,1:T(8,128)}, u32[]{:S(2)}) copy-start(s32[64,8]{0,1:T(8,128)} %param.7) | copy-start | bytes 6148
  50.2 15.4 %all-to-all-start = ((bf16[8,16,32,128]{3,2,1,0:T(8,128)(2,1)}), bf16[8,16,32,128]{3,2,1,0:T(8,128)(2,1)S(1)}, u32[]{:S(2)}, u32[]{:S(2)}) async-start(bf16[8,16,32,128]{3,2,1,0:T(8,128)(2,1)} %broadcast_in_dim.37), calls=%async_computation | async-start | bytes 2097152 | tf_op jit(solution)/shard_map/all_to_all | solution.py:16
  127.9 1.5 %copy-start.3 = (bf16[16384,56]{0,1:T(8,128)(2,1)S(1)}, bf16[16384,56]{0,1:T(8,128)(2,1)}, u32[]{:S(2)}) copy-start(bf16[16384,56]{0,1:T(8,128)(2,1)} %param.11) | copy-start | bytes 5505028

commit v2 on v1

v2 whole, which is shorter than its diff:
```python
import jax
import jax.numpy as jnp
from jax import lax
from jax.experimental import pallas as pl
from jax.experimental.pallas import tpu as pltpu
from jax.sharding import Mesh
from jax.sharding import PartitionSpec as P

HIDDEN_SIZE = 1024
EXPERTS = 16
SLOTS = 40
NEAR_SIZE = 8
GROUP = ("expert_0", "expert_1", "expert_2")
NEAR = ("expert_1", "expert_2")
LIMIT = pltpu.CompilerParams(vmem_limit_bytes=32 * 2**20)
F32 = jnp.float32
BF16 = jnp.bfloat16


def dot(x, y, x_dim, y_dim):
    return lax.dot_general(x, y, (((x_dim,), (y_dim,)), ((), ())), preferred_element_type=F32)


def pack_kernel(columns, packed):
    packed[:, :64] = columns[:32]
    packed[:24, 64:] = columns[32:]
    packed[24:, 64:] = jnp.zeros((8, 64), BF16)


def gates_kernel(parts, gate, up, weights, place, pieces):
    low = jnp.zeros((128, 256), F32)
    high = jnp.zeros((128, 256), F32)
    for near in range(NEAR_SIZE):
        x = parts[near].reshape(512, 128)
        w = [ref[:, near, :32, :].reshape(512, 128) for ref in (gate, up)]
        low = low + dot(x, jnp.concatenate(w, axis=1), 0, 0)
        x = parts[near, :, :24, :].reshape(384, 128)
        w = [ref[:, near, 32:, :].reshape(384, 128) for ref in (gate, up)]
        high = high + dot(x, jnp.concatenate(w, axis=1), 0, 0)
    both = low[:64] + high[64:]
    gate_proj, up_proj = both[:, :128], both[:, 128:]
    silu = gate_proj / (1.0 + jnp.exp(-gate_proj))
    hidden = (silu * up_proj * weights[...]).astype(BF16)
    pieces[...] = dot(place[...], hidden, 1, 0).astype(BF16)


def down_kernel(gathered, down, place, out):
    total = jnp.zeros((56, 64), F32)
    for expert in range(EXPERTS):
        for near in range(0, NEAR_SIZE, 2):
            pair = [gathered[near, expert], gathered[near + 1, expert]]
            hidden = dot(place[expert], jnp.concatenate(pair, axis=1), 0, 0).astype(BF16)
            low = expert * HIDDEN_SIZE + near * 128
            total = total + dot(down[:, low : low + 256], hidden, 1, 1)
    out[...] = total.astype(BF16)


def call(kernel, shape, name, *args):
    out = jax.ShapeDtypeStruct(shape, BF16)
    return pl.pallas_call(kernel, out_shape=out, compiler_params=LIMIT, name=name)(*args)


def spread(x):
    far = lax.all_gather(x[None], "expert_0", tiled=True)
    near = jnp.broadcast_to(far[None], (NEAR_SIZE, *far.shape))
    return lax.all_to_all(near, NEAR, 0, 0)


def body(tokens, routes, gate_values, gate_weight, up_weight, down_weight):
    expert = lax.axis_index("expert_0")
    packed = call(pack_kernel, (32, 128), "pack", tokens.T)
    parts = spread(packed)

    matched = routes[:, :, None] == lax.broadcasted_iota(jnp.int32, (1, 1, EXPERTS), 2)
    combine_table = jnp.sum(jnp.where(matched, gate_values[:, :, None].astype(F32), 0.0), axis=1)
    weights = lax.dynamic_slice_in_dim(combine_table, expert, 1, 1)
    present = jnp.any(matched, axis=1)
    slot = jnp.cumsum(present.astype(jnp.int32), axis=0) - 1
    place = jnp.logical_and(
        present.T[:, None, :],
        slot.T[:, None, :] == lax.broadcasted_iota(jnp.int32, (1, SLOTS, 1), 1),
    ).astype(BF16)
    own = lax.dynamic_slice_in_dim(place, expert, 1, 0)[0]

    shape = (EXPERTS, NEAR_SIZE, 56, 128)
    pieces = call(
        gates_kernel, (SLOTS, 128), "gates",
        parts, gate_weight.reshape(shape), up_weight.reshape(shape), weights, own,
    )
    gathered = spread(pieces)
    return call(down_kernel, (56, 64), "down", gathered, down_weight.T, place).T


def solution(mesh):
    split = Mesh(mesh.devices.reshape(mesh.shape["dp"], EXPERTS, 2, 4), ("dp", *GROUP))
    return jax.shard_map(
        body,
        mesh=split,
        in_specs=(
            P("dp", GROUP),
            P("dp", None),
            P("dp", None),
            P(None, GROUP),
            P(None, GROUP),
            P(None, GROUP),
        ),
        out_specs=P("dp", GROUP),
        check_vma=False,
    )
```

time: 133 us -> 119 us (0.89)
  local copies, waits for them, and re-layouts: 13.2 us -> 3.83 us
  matrix products: 6.03 us -> 0 us
  Pallas kernels: 0 us -> 3.3 us
  other arithmetic: 1.88 us -> 0.21 us
    dot_general x4 -> x0, matrix products: 6.03 us -> none  [the longest x1 2.75 us: body(): result = jnp.dot(full, down_weight, preferred_element_type=jnp.float32)]
    concatenate x1 -> x0, local copies, waits for them, and re-layouts: 4.42 us -> none  [body(): features = jnp.concatenate([parts[..., :64], parts[:, :, :24, 64:]], axis=2)]
    reshape x1 -> x0, local copies, waits for them, and re-layouts: 3.98 us -> none  [body(): features = features.reshape(-1, token_count)]
    pallas_call x0 -> x3, Pallas kernels: none -> 3.3 us  [call(): pl.pallas_call(kernel, out_shape=out, compiler_params=LIMIT, name=name)]
    unnamed x8 -> x13, local copies, waits for them, and re-layouts: 0.15 us -> 2.32 us
    slice x3 -> x0, local copies, waits for them, and re-layouts: 1.81 us -> none  [the longest x1 0.83 us: body(): columns[32:]]
    concatenate x2 -> x0, other arithmetic: 1.68 us -> none  [the longest x1 1.6 us: body(): features = jnp.concatenate([parts[..., :64], parts[:, :, :24, 64:]], axis=2)]
    convert_element_type x1 -> x0, local copies, waits for them, and re-layouts: 1.35 us -> none  [body(): full = lax.dot_general(placement, gathered, (((2,), (2,)), ((1,), (1,))),...]
where the time goes in v2:
time: 119 us; the launch traced here: 118 us
  blocking collectives  96.1 us (81%)
  waiting for transfers between devices  10.1 us (8%)
  starting transfers between devices  4.84 us (4%)
  local copies, waits for them, and re-layouts  3.83 us (3%)
  Pallas kernels  3.3 us (3%)
    all_gather x2, blocking collectives, spread(): far = lax.all_gather(x[None], 'expert_0', tiled=True)  79.6 us
    all_to_all x1, blocking collectives, spread(): return lax.all_to_all(near, NEAR, 0, 0)  16.5 us
    all_to_all x1, waiting for transfers between devices, spread(): return lax.all_to_all(near, NEAR, 0, 0)  10.1 us
    all_to_all x1, starting transfers between devices, spread(): return lax.all_to_all(near, NEAR, 0, 0)  4.84 us
    pallas_call x3, Pallas kernels, call(): pl.pallas_call(kernel, out_shape=out, compiler_params=LIMIT, name=name)  3.3 us
  transfers between devices with their start and end apart: 1, of which 1 were waited for; matrix products, arithmetic and copies ran while one was open for 0% of the time, Pallas kernels for 0%

profile of v2, /device:TPU:6, one launch (start us, length us, event | category | flops | bytes accessed | tf_op | source)
XLA Modules:
  0.0 118.4 jit_solution(7953102062532625215)
XLA Ops:
  0.0 0.0 copy-start.3
  0.0 0.7 copy-done.3
  0.7 0.0 copy-start.5
  0.7 0.0 copy-start.4
  0.7 0.1 pack.1
  0.8 47.5 %all-gather = bf16[512,128]{1,0:T(8,128)(2,1)S(1)} all-gather(bf16[32,128]{1,0:T(8,128)(2,1)S(1)} %pack.1), channel_id=2, replica_groups=mesh['dp'=8,'expert_0'=16,'expert_1'=2,'expert_2'=4] {'expert_0'}, dimensions={0}, use_global_device_ids=true | all-gather | bytes 139264 | tf_op jit(solution)/shard_map/all_gather | solution.py:64
  48.3 0.0 copy-start
  48.3 1.2 broadcast_in_dim.21
  49.4 4.8 %all-to-all-start = ((bf16[8,16,32,128]{3,2,1,0:T(8,128)(2,1)}), bf16[8,16,32,128]{3,2,1,0:T(8,128)(2,1)S(1)}, u32[]{:S(2)}, u32[]{:S(2)}) async-start(bf16[8,16,32,128]{3,2,1,0:T(8,128)(2,1)} %broadcast_in_dim.21), calls=%async_computation | async-start | bytes 2097152 | tf_op jit(solution)/shard_map/all_to_all | solution.py:66
  54.3 0.0 copy-done.5
  54.3 0.0 copy-done.4
  54.3 0.1 copy.12
  54.4 0.1 reduce_window_sum.11
  54.5 0.1 copy.13
  54.6 0.1 copy.14.weights
  54.7 0.1 fusion.1.place
  54.8 10.1 %all-to-all-done.parts = bf16[8,16,32,128]{3,2,1,0:T(8,128)(2,1)S(1)} async-done(((bf16[8,16,32,128]{3,2,1,0:T(8,128)(2,1)}), bf16[8,16,32,128]{3,2,1,0:T(8,128)(2,1)S(1)}, u32[]{:S(2)}, u32[]{:S(2)}) %all-to-all-start) | async-done | bytes 1048608 | tf_op jit(solution)/shard_map/all_to_all | solution.py:66
  64.9 0.0 copy-done
  64.9 0.0 copy-start.1
  64.9 1.5 %copy-done.1 = bf16[7168,128]{1,0:T(8,128)(2,1)S(1)} copy-done((bf16[7168,128]{1,0:T(8,128)(2,1)S(1)}, bf16[7168,128]{1,0:T(8,128)(2,1)}, u32[]{:S(2)}) %copy-start.1) | copy-done | bytes 1835032
  66.4 1.1 gates.1
  67.5 32.1 %all-gather.1 = bf16[640,128]{1,0:T(8,128)(2,1)S(1)} all-gather(bf16[40,128]{1,0:T(8,128)(2,1)S(1)} %gates.1), channel_id=3, replica_groups=mesh['dp'=8,'expert_0'=16,'expert_1'=2,'expert_2'=4] {'expert_0'}, dimensions={0}, use_global_device_ids=true | all-gather | bytes 174080 | tf_op jit(solution)/shard_map/all_gather | solution.py:64
  99.6 0.0 copy-start.2
  99.6 0.2 broadcast_in_dim.39
  99.8 16.5 %all_to_all.10.gathered = bf16[8,16,40,128]{3,2,1,0:T(8,128)(2,1)S(1)} all-to-all(bf16[8,16,40,128]{3,2,1,0:T(8,128)(2,1)S(1)} %broadcast_in_dim.39), channel_id=1, replica_groups=mesh['dp'=8,'expert_0'=16,'expert_1'=2,'expert_2'=4] {'expert_1','expert..., dimensions={0} | all-to-all | bytes 2621440 | tf_op jit(solution)/shard_map/all_to_all | solution.py:66
  116.3 0.0 copy-done.2
  116.3 2.1 %down.1 = bf16[56,64]{1,0:T(8,128)(2,1)} custom-call(bf16[8,16,40,128]{3,2,1,0:T(8,128)(2,1)S(1)} %all_to_all.10.gathered, bf16[56,16384]{1,0:T(8,128)(2,1)S(1)} %bitcast.14, bf16[16,40,64]{2,1,0:T(8,128)(2,1)S(1)} %fusion.1.place), custom_call_target="tpu_custom_call" | custom-call | tf_op jit(solution)/shard_map/down/pallas_call | solution.py:60
  (7 shorter events, 0.1 us)
Async XLA Ops:
  0.0 0.7 copy-start.3
  0.7 53.6 %copy-start.5 = (bf16[64,8]{0,1:T(8,128)(2,1)S(1)}, bf16[64,8]{0,1:T(8,128)(2,1)}, u32[]{:S(2)}) copy-start(bf16[64,8]{0,1:T(8,128)(2,1)} %param.8) | copy-start | bytes 3076
  0.7 53.6 %copy-start.4 = (s32[64,8]{0,1:T(8,128)S(1)}, s32[64,8]{0,1:T(8,128)}, u32[]{:S(2)}) copy-start(s32[64,8]{0,1:T(8,128)} %param.7) | copy-start | bytes 6148
  48.3 16.6 %copy-start = (bf16[7168,128]{1,0:T(8,128)(2,1)S(1)}, bf16[7168,128]{1,0:T(8,128)(2,1)}, u32[]{:S(2)}) copy-start(bf16[7168,128]{1,0:T(8,128)(2,1)} %param.9) | copy-start | bytes 5505028
  49.4 15.4 %all-to-all-start = ((bf16[8,16,32,128]{3,2,1,0:T(8,128)(2,1)}), bf16[8,16,32,128]{3,2,1,0:T(8,128)(2,1)S(1)}, u32[]{:S(2)}, u32[]{:S(2)}) async-start(bf16[8,16,32,128]{3,2,1,0:T(8,128)(2,1)} %broadcast_in_dim.21), calls=%async_computation | async-start | bytes 2097152 | tf_op jit(solution)/shard_map/all_to_all | solution.py:66
  64.9 1.5 %copy-start.1 = (bf16[7168,128]{1,0:T(8,128)(2,1)S(1)}, bf16[7168,128]{1,0:T(8,128)(2,1)}, u32[]{:S(2)}) copy-start(bf16[7168,128]{1,0:T(8,128)(2,1)} %param.10) | copy-start | bytes 5505028
  99.6 16.7 %copy-start.2 = (bf16[16384,56]{0,1:T(8,128)(2,1)S(1)}, bf16[16384,56]{0,1:T(8,128)(2,1)}, u32[]{:S(2)}) copy-start(bf16[16384,56]{0,1:T(8,128)(2,1)} %param.11) | copy-start | bytes 5505028

commit v3 on v2

v3 whole, which is shorter than its diff:
```python
import jax
import jax.numpy as jnp
from jax import lax
from jax.experimental import pallas as pl
from jax.experimental.pallas import tpu as pltpu
from jax.sharding import Mesh
from jax.sharding import PartitionSpec as P

HIDDEN_SIZE = 1024
EXPERTS = 16
TOPK = 8
TOKENS = 64
SLOTS = 40
FEATURES = 56
NEAR_SIZE = 8
TALL = EXPERTS * FEATURES
ROWS = 304
GROUP = ("expert_0", "expert_1", "expert_2")
NEAR = ("expert_1", "expert_2")
LIMIT = pltpu.CompilerParams(vmem_limit_bytes=8 * 2**20)
VMEM = pl.BlockSpec(memory_space=pltpu.VMEM)
SMEM = pl.BlockSpec(memory_space=pltpu.SMEM)
COST = pl.CostEstimate(flops=10**10, bytes_accessed=6 * 10**7, transcendentals=0)
F32 = jnp.float32
BF16 = jnp.bfloat16


def dot(x, y, x_dim, y_dim):
    return lax.dot_general(x, y, (((x_dim,), (y_dim,)), ((), ())), preferred_element_type=F32)


def span(group):
    return group * ROWS, min((group + 1) * ROWS, TALL)


def pack_kernel(columns, packed):
    packed[:, :64] = columns[:32]
    packed[:24, 64:] = columns[32:]
    packed[24:, 64:] = jnp.zeros((8, 64), BF16)


def route(expert, routes, values, place, weights):
    earlier = lax.broadcasted_iota(jnp.int32, (TOKENS, TOKENS), 0)
    earlier = earlier < lax.broadcasted_iota(jnp.int32, (TOKENS, TOKENS), 1)
    earlier = jnp.where(earlier, 1.0, 0.0).astype(BF16)
    ids = lax.broadcasted_iota(jnp.int32, (EXPERTS, TOKENS), 0)
    slots = lax.broadcasted_iota(jnp.int32, (SLOTS, TOKENS), 0).astype(F32)
    table = jnp.zeros((EXPERTS, TOKENS), F32)
    present = jnp.zeros((EXPERTS, TOKENS), F32)
    for k in range(TOPK):
        matched = routes[k : k + 1, :] == ids
        table = jnp.where(matched, values[k : k + 1, :].astype(F32), table)
        present = jnp.where(matched, 1.0, present)
    slot = dot(present.astype(BF16), earlier, 1, 0)
    slot = jnp.where(present > 0.0, slot, -1.0)
    for e in range(EXPERTS):
        chosen = jnp.where(slot[e : e + 1, :] == slots, 1.0, 0.0)
        place[e * SLOTS : (e + 1) * SLOTS, :] = chosen.astype(BF16)
    mine = ids == expert
    own_slot = jnp.sum(jnp.where(mine, slot, 0.0), axis=0, keepdims=True)
    own_gate = jnp.sum(jnp.where(mine, table, 0.0), axis=0, keepdims=True)
    chosen = jnp.where(own_slot == slots, 1.0, 0.0)
    weights[...] = jnp.sum(chosen * own_gate, axis=1, keepdims=True)
    return chosen.astype(BF16)


def pick_kernel(expert, routes, values, far, out, place, weights):
    own = route(expert[0], routes, values, place, weights)
    blank = jnp.zeros((SLOTS, 64), BF16)
    halves = jnp.concatenate([own, blank], axis=1), jnp.concatenate([blank, own], axis=1)
    total = jnp.zeros((ROWS, 128), F32)
    for group in range(3):
        first, last = span(group)
        low, high = first // FEATURES, -(-last // FEATURES)
        above, below = group * SLOTS, 128 - (group + 1) * SLOTS
        sides = []
        for half in halves:
            chooser = [half, jnp.zeros((below, 128), BF16)]
            if above:
                chooser = [jnp.zeros((above, 128), BF16), *chooser]
            chooser = jnp.concatenate(chooser, axis=0)
            sides.append(dot(far[low * 32 : high * 32, :], chooser, 1, 1))
        rows = []
        for piece in range(low, high):
            for side, (start, stop) in enumerate(((0, 32), (32, FEATURES))):
                begin = max(first - piece * FEATURES, start)
                end = min(last - piece * FEATURES, stop)
                if begin < end:
                    base = (piece - low) * 32 - start
                    rows.append(sides[side][base + begin : base + end])
        if last - first < ROWS:
            rows.append(jnp.zeros((ROWS - (last - first), 128), F32))
        total = total + jnp.concatenate(rows, axis=0)
    result = total.astype(BF16)
    for near in range(NEAR_SIZE):
        out[near] = result


def gates_kernel(parts, gate, up, weights, pieces):
    totals = [jnp.zeros((128, 256), F32)] * 3
    for near in range(NEAR_SIZE):
        x = parts[near]
        w = [ref[:, near, :, :].reshape(TALL, 128) for ref in (gate, up)]
        w = jnp.concatenate(w, axis=1)
        for group in range(3):
            first, last = span(group)
            totals[group] = totals[group] + dot(x[: last - first], w[first:last], 0, 0)
    both = [totals[group][group * SLOTS : (group + 1) * SLOTS] for group in range(3)]
    both = both[0] + both[1] + both[2]
    gate_proj, up_proj = both[:, :128], both[:, 128:]
    silu = gate_proj / (1.0 + jnp.exp(-gate_proj))
    pieces[...] = (silu * up_proj * weights[...]).astype(BF16)


def down_kernel(gathered, down, place, out):
    rows = []
    for expert in range(EXPERTS):
        total = jnp.zeros((SLOTS, FEATURES), F32)
        for near in range(0, NEAR_SIZE, 2):
            pair = [gathered[near, expert], gathered[near + 1, expert]]
            low = expert * HIDDEN_SIZE + near * 128
            total = total + dot(jnp.concatenate(pair, axis=1), down[:, low : low + 256], 1, 1)
        rows.append(total)
    rows = jnp.concatenate(rows, axis=0)
    coarse = rows.astype(BF16)
    fine = (rows - coarse.astype(F32)).astype(BF16)
    out[...] = (dot(coarse, place[...], 0, 0) + dot(fine, place[...], 0, 0)).astype(BF16)


def call(kernel, name, shapes, args, **options):
    out = [jax.ShapeDtypeStruct(shape, dtype) for shape, dtype in shapes]
    return pl.pallas_call(kernel, out_shape=out, compiler_params=LIMIT, cost_estimate=COST, name=name, **options)(*args)


def body(tokens, routes, gate_values, gate_weight, up_weight, down_weight):
    expert = lax.axis_index("expert_0").reshape(1)
    (packed,) = call(pack_kernel, "pack", [((32, 128), BF16)], (tokens.T,))
    far = lax.all_gather(packed, "expert_0", tiled=True)
    near, place, weights = call(
        pick_kernel,
        "pick",
        [((NEAR_SIZE, ROWS, 128), BF16), ((EXPERTS * SLOTS, TOKENS), BF16), ((SLOTS, 1), F32)],
        (expert, routes.T, gate_values.T, far),
        in_specs=[SMEM, VMEM, VMEM, VMEM],
    )
    parts = lax.all_to_all(near, NEAR, 0, 0)
    shape = (EXPERTS, NEAR_SIZE, FEATURES, 128)
    (pieces,) = call(
        gates_kernel,
        "gates",
        [((SLOTS, 128), BF16)],
        (parts, gate_weight.reshape(shape), up_weight.reshape(shape), weights),
    )
    far = lax.all_gather(pieces[None], "expert_0", tiled=True)
    near = jnp.broadcast_to(far[None], (NEAR_SIZE, *far.shape))
    gathered = lax.all_to_all(near, NEAR, 0, 0)
    (out,) = call(
        down_kernel, "down", [((FEATURES, TOKENS), BF16)], (gathered, down_weight.T, place)
    )
    return out.T


def solution(mesh):
    split = Mesh(mesh.devices.reshape(mesh.shape["dp"], EXPERTS, 2, 4), ("dp", *GROUP))
    return jax.shard_map(
        body,
        mesh=split,
        in_specs=(
            P("dp", GROUP),
            P("dp", None),
            P("dp", None),
            P(None, GROUP),
            P(None, GROUP),
            P(None, GROUP),
        ),
        out_specs=P("dp", GROUP),
        check_vma=False,
    )
```

time: 119 us -> 114 us (0.958)
  blocking collectives: 96.1 us -> 109 us
  waiting for transfers between devices: 10.1 us -> 0 us
  starting transfers between devices: 4.84 us -> 0 us
  local copies, waits for them, and re-layouts: 3.83 us -> 0.9 us
    all_to_all x1 -> x2, blocking collectives: 16.5 us -> 29.9 us  [the longest x1 15.5 us: body(): gathered = lax.all_to_all(near, NEAR, 0, 0)]
    all_to_all x1 -> x0, waiting for transfers between devices: 10.1 us -> none  [spread(): return lax.all_to_all(near, NEAR, 0, 0)]
    all_to_all x1 -> x0, starting transfers between devices: 4.84 us -> none  [spread(): return lax.all_to_all(near, NEAR, 0, 0)]
    unnamed x13 -> x12, local copies, waits for them, and re-layouts: 2.32 us -> 0.73 us
    pallas_call x3 -> x4, Pallas kernels: 3.3 us -> 3.13 us  [call(): pl.pallas_call(kernel, out_shape=out, compiler_params=LIMIT, cost_estimat...]
  transfers between devices with their start and end apart: 1 -> 0, of which waited for: 1 -> 0; matrix products, arithmetic and copies ran while one was open for 0% -> 0% of each run, Pallas kernels for 0% -> 0%
where the time goes in v3:
time: 114 us
  blocking collectives  109 us (96%)
  Pallas kernels  3.13 us (3%)
    all_gather x1, blocking collectives, body(): far = lax.all_gather(packed, 'expert_0', tiled=True)  47.5 us
    all_gather x1, blocking collectives, body(): far = lax.all_gather(pieces[None], 'expert_0', tiled=True)  32.1 us
    all_to_all x1, blocking collectives, body(): gathered = lax.all_to_all(near, NEAR, 0, 0)  15.5 us
    all_to_all x1, blocking collectives, body(): parts = lax.all_to_all(near, NEAR, 0, 0)  14.3 us
    pallas_call x4, Pallas kernels, call(): pl.pallas_call(kernel, out_shape=out, compiler_params=LIMIT, cost_estimat...  3.13 us

profile of v3, /device:TPU:6, one launch (start us, length us, event | category | flops | bytes accessed | tf_op | source)
XLA Modules:
  0.0 113.5 jit_solution(3353450036709909354)
XLA Ops:
  0.0 0.0 copy-start.3
  0.0 0.7 copy-done.3
  0.7 0.0 copy-start.4
  0.7 0.0 copy-start.5
  0.7 0.1 pack.1
  0.8 47.5 %all_gather.6.far = bf16[512,128]{1,0:T(8,128)(2,1)S(1)} all-gather(bf16[32,128]{1,0:T(8,128)(2,1)S(1)} %pack.1), channel_id=1, replica_groups=mesh['dp'=8,'expert_0'=16,'expert_1'=2,'expert_2'=4] {'expert_0'}, dimensions={0}, use_global_device_ids=true | all-gather | bytes 139264 | tf_op jit(solution)/shard_map/all_gather | solution.py:138
  48.3 0.0 copy-done.4
  48.3 0.0 copy-done.5
  48.3 0.0 copy-start
  48.3 0.0 copy-start.1
  48.3 0.5 pick.1
  48.7 14.3 %all_to_all.10.parts = bf16[8,304,128]{2,1,0:T(8,128)(2,1)S(1)} all-to-all(bf16[8,304,128]{2,1,0:T(8,128)(2,1)S(1)} %get-tuple-element.8), channel_id=1, replica_groups=mesh['dp'=8,'expert_0'=16,'expert_1'=2,'expert_2'=4] {'expert_1','expert..., dimensions={0} | all-to-all | bytes 1245184 | tf_op jit(solution)/shard_map/all_to_all | solution.py:146
  63.1 0.0 copy-done
  63.1 0.0 copy-done.1
  63.1 1.1 gates.1
  64.2 32.1 %all-gather = bf16[640,128]{1,0:T(8,128)(2,1)S(1)} all-gather(bf16[40,128]{1,0:T(8,128)(2,1)S(1)} %gates.1), channel_id=2, replica_groups=mesh['dp'=8,'expert_0'=16,'expert_1'=2,'expert_2'=4] {'expert_0'}, dimensions={0}, use_global_device_ids=true | all-gather | bytes 174080 | tf_op jit(solution)/shard_map/all_gather | solution.py:154
  96.3 0.0 copy-start.2
  96.3 0.2 broadcast_in_dim.10
  96.5 15.5 %all_to_all.11.gathered = bf16[8,16,40,128]{3,2,1,0:T(8,128)(2,1)S(1)} all-to-all(bf16[8,16,40,128]{3,2,1,0:T(8,128)(2,1)S(1)} %broadcast_in_dim.10), channel_id=1, replica_groups=mesh['dp'=8,'expert_0'=16,'expert_1'=2,'expert_2'=4] {'expert_1','expert..., dimensions={0} | all-to-all | bytes 2621440 | tf_op jit(solution)/shard_map/all_to_all | solution.py:156
  112.0 0.0 copy-done.2
  112.0 1.5 %down.1 = bf16[56,64]{1,0:T(8,128)(2,1)} custom-call(bf16[8,16,40,128]{3,2,1,0:T(8,128)(2,1)S(1)} %all_to_all.11.gathered, bf16[56,16384]{1,0:T(8,128)(2,1)S(1)} %bitcast.11, bf16[640,64]{1,0:T(8,128)(2,1)S(1)} %get-tuple-element.10.place), custom_call_target="tpu_custom_call" | custom-call | flops 10000000000 | bytes 60000000 | tf_op jit(solution)/shard_map/down/pallas_call | solution.py:132
Async XLA Ops:
  0.0 0.7 copy-start.3
  0.7 47.5 %copy-start.4 = (s32[64,8]{0,1:T(8,128)S(1)}, s32[64,8]{0,1:T(8,128)}, u32[]{:S(2)}) copy-start(s32[64,8]{0,1:T(8,128)} %param.7) | copy-start | bytes 6148
  0.7 47.6 %copy-start.5 = (bf16[64,8]{0,1:T(8,128)(2,1)S(1)}, bf16[64,8]{0,1:T(8,128)(2,1)}, u32[]{:S(2)}) copy-start(bf16[64,8]{0,1:T(8,128)(2,1)} %param.8) | copy-start | bytes 3076
  48.3 14.8 %copy-start = (bf16[7168,128]{1,0:T(8,128)(2,1)S(1)}, bf16[7168,128]{1,0:T(8,128)(2,1)}, u32[]{:S(2)}) copy-start(bf16[7168,128]{1,0:T(8,128)(2,1)} %param.9) | copy-start | bytes 5505028
  48.3 14.8 %copy-start.1 = (bf16[7168,128]{1,0:T(8,128)(2,1)S(1)}, bf16[7168,128]{1,0:T(8,128)(2,1)}, u32[]{:S(2)}) copy-start(bf16[7168,128]{1,0:T(8,128)(2,1)} %param.10) | copy-start | bytes 5505028
  96.3 15.7 %copy-start.2 = (bf16[16384,56]{0,1:T(8,128)(2,1)S(1)}, bf16[16384,56]{0,1:T(8,128)(2,1)}, u32[]{:S(2)}) copy-start(bf16[16384,56]{0,1:T(8,128)(2,1)} %param.11) | copy-start | bytes 5505028

commit v4 on v3

--- a/solution.py
+++ b/solution.py
@@ -14,7 +14,7 @@
 FEATURES = 56
 NEAR_SIZE = 8
 TALL = EXPERTS * FEATURES
-ROWS = 304
+SPLIT = 32
 GROUP = ("expert_0", "expert_1", "expert_2")
 NEAR = ("expert_1", "expert_2")
 LIMIT = pltpu.CompilerParams(vmem_limit_bytes=8 * 2**20)
@@ -29,14 +29,10 @@
     return lax.dot_general(x, y, (((x_dim,), (y_dim,)), ((), ())), preferred_element_type=F32)
 
 
-def span(group):
-    return group * ROWS, min((group + 1) * ROWS, TALL)
-
-
 def pack_kernel(columns, packed):
-    packed[:, :64] = columns[:32]
-    packed[:24, 64:] = columns[32:]
-    packed[24:, 64:] = jnp.zeros((8, 64), BF16)
+    packed[:, :64] = columns[:SPLIT]
+    packed[: FEATURES - SPLIT, 64:] = columns[SPLIT:]
+    packed[FEATURES - SPLIT :, 64:] = jnp.zeros((2 * SPLIT - FEATURES, 64), BF16)
 
 
 def route(expert, routes, values, place, weights):
@@ -67,47 +63,22 @@
 def pick_kernel(expert, routes, values, far, out, place, weights):
     own = route(expert[0], routes, values, place, weights)
     blank = jnp.zeros((SLOTS, 64), BF16)
-    halves = jnp.concatenate([own, blank], axis=1), jnp.concatenate([blank, own], axis=1)
-    total = jnp.zeros((ROWS, 128), F32)
-    for group in range(3):
-        first, last = span(group)
-        low, high = first // FEATURES, -(-last // FEATURES)
-        above, below = group * SLOTS, 128 - (group + 1) * SLOTS
-        sides = []
-        for half in halves:
-            chooser = [half, jnp.zeros((below, 128), BF16)]
-            if above:
-                chooser = [jnp.zeros((above, 128), BF16), *chooser]
-            chooser = jnp.concatenate(chooser, axis=0)
-            sides.append(dot(far[low * 32 : high * 32, :], chooser, 1, 1))
-        rows = []
-        for piece in range(low, high):
-            for side, (start, stop) in enumerate(((0, 32), (32, FEATURES))):
-                begin = max(first - piece * FEATURES, start)
-                end = min(last - piece * FEATURES, stop)
-                if begin < end:
-                    base = (piece - low) * 32 - start
-                    rows.append(sides[side][base + begin : base + end])
-        if last - first < ROWS:
-            rows.append(jnp.zeros((ROWS - (last - first), 128), F32))
-        total = total + jnp.concatenate(rows, axis=0)
-    result = total.astype(BF16)
+    low = dot(jnp.concatenate([own, blank], axis=1), far[...].reshape(EXPERTS * SPLIT, 128), 1, 1)
+    high = far[:, : FEATURES - SPLIT, :].reshape(EXPERTS * (FEATURES - SPLIT), 128)
+    high = dot(jnp.concatenate([blank, own], axis=1), high, 1, 1)
+    picked = jnp.concatenate([low, high], axis=1).astype(BF16)
     for near in range(NEAR_SIZE):
-        out[near] = result
+        out[near] = picked
 
 
 def gates_kernel(parts, gate, up, weights, pieces):
-    totals = [jnp.zeros((128, 256), F32)] * 3
+    total = jnp.zeros((SLOTS, 256), F32)
     for near in range(NEAR_SIZE):
-        x = parts[near]
-        w = [ref[:, near, :, :].reshape(TALL, 128) for ref in (gate, up)]
-        w = jnp.concatenate(w, axis=1)
-        for group in range(3):
-            first, last = span(group)
-            totals[group] = totals[group] + dot(x[: last - first], w[first:last], 0, 0)
-    both = [totals[group][group * SLOTS : (group + 1) * SLOTS] for group in range(3)]
-    both = both[0] + both[1] + both[2]
-    gate_proj, up_proj = both[:, :128], both[:, 128:]
+        w = [ref[:, near, :SPLIT, :].reshape(EXPERTS * SPLIT, 128) for ref in (gate, up)]
+        total = total + dot(parts[near, :, : EXPERTS * SPLIT], jnp.concatenate(w, axis=1), 1, 0)
+        w = [ref[:, near, SPLIT:, :].reshape(TALL - EXPERTS * SPLIT, 128) for ref in (gate, up)]
+        total = total + dot(parts[near, :, EXPERTS * SPLIT :], jnp.concatenate(w, axis=1), 1, 0)
+    gate_proj, up_proj = total[:, :128], total[:, 128:]
     silu = gate_proj / (1.0 + jnp.exp(-gate_proj))
     pieces[...] = (silu * up_proj * weights[...]).astype(BF16)
 
@@ -129,17 +100,19 @@
 
 def call(kernel, name, shapes, args, **options):
     out = [jax.ShapeDtypeStruct(shape, dtype) for shape, dtype in shapes]
-    return pl.pallas_call(kernel, out_shape=out, compiler_params=LIMIT, cost_estimate=COST, name=name, **options)(*args)
+    return pl.pallas_call(
+        kernel, out_shape=out, compiler_params=LIMIT, cost_estimate=COST, name=name, **options
+    )(*args)
 
 
 def body(tokens, routes, gate_values, gate_weight, up_weight, down_weight):
     expert = lax.axis_index("expert_0").reshape(1)
-    (packed,) = call(pack_kernel, "pack", [((32, 128), BF16)], (tokens.T,))
-    far = lax.all_gather(packed, "expert_0", tiled=True)
+    (packed,) = call(pack_kernel, "pack", [((SPLIT, 128), BF16)], (tokens.T,))
+    far = lax.all_gather(packed[None], "expert_0", tiled=True)
     near, place, weights = call(
         pick_kernel,
         "pick",
-        [((NEAR_SIZE, ROWS, 128), BF16), ((EXPERTS * SLOTS, TOKENS), BF16), ((SLOTS, 1), F32)],
+        [((NEAR_SIZE, SLOTS, TALL), BF16), ((EXPERTS * SLOTS, TOKENS), BF16), ((SLOTS, 1), F32)],
         (expert, routes.T, gate_values.T, far),
         in_specs=[SMEM, VMEM, VMEM, VMEM],
     )

time: 114 us -> 113 us (level)
  no operation moved by 1% of the time
where the time goes in v4:
time: 113 us
  blocking collectives  110 us (97%)
  Pallas kernels  2.61 us (2%)
    all_gather x1, blocking collectives, body(): far = lax.all_gather(packed[None], 'expert_0', tiled=True)  47.5 us
    all_gather x1, blocking collectives, body(): far = lax.all_gather(pieces[None], 'expert_0', tiled=True)  32.6 us
    all_to_all x1, blocking collectives, body(): gathered = lax.all_to_all(near, NEAR, 0, 0)  15.4 us
    all_to_all x1, blocking collectives, body(): parts = lax.all_to_all(near, NEAR, 0, 0)  14.1 us
    pallas_call x4, Pallas kernels, call(): pl.pallas_call(kernel, out_shape=out, compiler_params=LIMIT, cost_estimat...  2.61 us

profile of v4, /device:TPU:6, one launch (start us, length us, event | category | flops | bytes accessed | tf_op | source)
XLA Modules:
  0.0 113.1 jit_solution(12348290886815040067)
XLA Ops:
  0.0 0.0 copy-start.3
  0.0 0.7 copy-done.3
  0.7 0.0 copy-start.4
  0.7 0.0 copy-start.5
  0.7 0.1 pack.1
  0.8 47.5 %all-gather = bf16[512,128]{1,0:T(8,128)(2,1)S(1)} all-gather(bf16[32,128]{1,0:T(8,128)(2,1)S(1)} %pack.1), channel_id=2, replica_groups=mesh['dp'=8,'expert_0'=16,'expert_1'=2,'expert_2'=4] {'expert_0'}, dimensions={0}, use_global_device_ids=true | all-gather | bytes 139264 | tf_op jit(solution)/shard_map/all_gather | solution.py:111
  48.3 0.0 copy-done.4
  48.3 0.0 copy-done.5
  48.3 0.0 copy-start
  48.3 0.0 copy-start.1
  48.3 0.4 pick.1
  48.7 14.1 %all_to_all.10.parts = bf16[8,40,896]{2,1,0:T(8,128)(2,1)S(1)} all-to-all(bf16[8,40,896]{2,1,0:T(8,128)(2,1)S(1)} %get-tuple-element.8), channel_id=1, replica_groups=mesh['dp'=8,'expert_0'=16,'expert_1'=2,'expert_2'=4] {'expert_1','expert..., dimensions={0} | all-to-all | bytes 1146880 | tf_op jit(solution)/shard_map/all_to_all | solution.py:119
  62.8 0.0 copy-done
  62.8 0.0 copy-done.1
  62.8 0.6 gates.1
  63.4 32.6 %all-gather.1 = bf16[640,128]{1,0:T(8,128)(2,1)S(1)} all-gather(bf16[40,128]{1,0:T(8,128)(2,1)S(1)} %gates.1), channel_id=3, replica_groups=mesh['dp'=8,'expert_0'=16,'expert_1'=2,'expert_2'=4] {'expert_0'}, dimensions={0}, use_global_device_ids=true | all-gather | bytes 174080 | tf_op jit(solution)/shard_map/all_gather | solution.py:127
  96.0 0.0 copy-start.2
  96.0 0.2 broadcast_in_dim.14
  96.2 15.4 %all_to_all.11.gathered = bf16[8,16,40,128]{3,2,1,0:T(8,128)(2,1)S(1)} all-to-all(bf16[8,16,40,128]{3,2,1,0:T(8,128)(2,1)S(1)} %broadcast_in_dim.14), channel_id=1, replica_groups=mesh['dp'=8,'expert_0'=16,'expert_1'=2,'expert_2'=4] {'expert_1','expert..., dimensions={0} | all-to-all | bytes 2621440 | tf_op jit(solution)/shard_map/all_to_all | solution.py:129
  111.6 0.0 copy-done.2
  111.6 1.5 %down.1 = bf16[56,64]{1,0:T(8,128)(2,1)} custom-call(bf16[8,16,40,128]{3,2,1,0:T(8,128)(2,1)S(1)} %all_to_all.11.gathered, bf16[56,16384]{1,0:T(8,128)(2,1)S(1)} %bitcast.13, bf16[640,64]{1,0:T(8,128)(2,1)S(1)} %get-tuple-element.10.place), custom_call_target="tpu_custom_call" | custom-call | flops 10000000000 | bytes 60000000 | tf_op jit(solution)/shard_map/down/pallas_call | solution.py:103
Async XLA Ops:
  0.0 0.7 copy-start.3
  0.7 47.5 %copy-start.4 = (s32[64,8]{0,1:T(8,128)S(1)}, s32[64,8]{0,1:T(8,128)}, u32[]{:S(2)}) copy-start(s32[64,8]{0,1:T(8,128)} %param.7) | copy-start | bytes 6148
  0.7 47.6 %copy-start.5 = (bf16[64,8]{0,1:T(8,128)(2,1)S(1)}, bf16[64,8]{0,1:T(8,128)(2,1)}, u32[]{:S(2)}) copy-start(bf16[64,8]{0,1:T(8,128)(2,1)} %param.8) | copy-start | bytes 3076
  48.3 14.5 %copy-start = (bf16[7168,128]{1,0:T(8,128)(2,1)S(1)}, bf16[7168,128]{1,0:T(8,128)(2,1)}, u32[]{:S(2)}) copy-start(bf16[7168,128]{1,0:T(8,128)(2,1)} %param.9) | copy-start | bytes 5505028
  48.3 14.5 %copy-start.1 = (bf16[7168,128]{1,0:T(8,128)(2,1)S(1)}, bf16[7168,128]{1,0:T(8,128)(2,1)}, u32[]{:S(2)}) copy-start(bf16[7168,128]{1,0:T(8,128)(2,1)} %param.10) | copy-start | bytes 5505028
  96.0 15.6 %copy-start.2 = (bf16[16384,56]{0,1:T(8,128)(2,1)S(1)}, bf16[16384,56]{0,1:T(8,128)(2,1)}, u32[]{:S(2)}) copy-start(bf16[16384,56]{0,1:T(8,128)(2,1)} %param.11) | copy-start | bytes 5505028

commit v5 on v4

--- a/solution.py
+++ b/solution.py
@@ -15,6 +15,8 @@
 NEAR_SIZE = 8
 TALL = EXPERTS * FEATURES
 SPLIT = 32
+FILLED = TOKENS * TOPK
+WINDOW = 48
 GROUP = ("expert_0", "expert_1", "expert_2")
 NEAR = ("expert_1", "expert_2")
 LIMIT = pltpu.CompilerParams(vmem_limit_bytes=8 * 2**20)
@@ -35,7 +37,7 @@
     packed[FEATURES - SPLIT :, 64:] = jnp.zeros((2 * SPLIT - FEATURES, 64), BF16)
 
 
-def route(expert, routes, values, place, weights):
+def route(expert, routes, values, place, weights, starts):
     earlier = lax.broadcasted_iota(jnp.int32, (TOKENS, TOKENS), 0)
     earlier = earlier < lax.broadcasted_iota(jnp.int32, (TOKENS, TOKENS), 1)
     earlier = jnp.where(earlier, 1.0, 0.0).astype(BF16)
@@ -49,9 +51,17 @@
         present = jnp.where(matched, 1.0, present)
     slot = dot(present.astype(BF16), earlier, 1, 0)
     slot = jnp.where(present > 0.0, slot, -1.0)
+    before = lax.broadcasted_iota(jnp.int32, (EXPERTS, EXPERTS), 0)
+    before = before > lax.broadcasted_iota(jnp.int32, (EXPERTS, EXPERTS), 1)
+    start = dot(jnp.where(before, 1.0, 0.0).astype(BF16), present.astype(BF16), 1, 0)
+    start = jnp.sum(start, axis=1, keepdims=True)
+    window = jnp.minimum(jnp.floor(start * 0.125) * 8.0, float(FILLED - WINDOW))
+    shifted = jnp.where(present > 0.0, slot + (start - window), -1.0)
+    rows = lax.broadcasted_iota(jnp.int32, (WINDOW, TOKENS), 0).astype(F32)
     for e in range(EXPERTS):
-        chosen = jnp.where(slot[e : e + 1, :] == slots, 1.0, 0.0)
-        place[e * SLOTS : (e + 1) * SLOTS, :] = chosen.astype(BF16)
+        chosen = jnp.where(shifted[e : e + 1, :] == rows, 1.0, 0.0)
+        place[e * WINDOW : (e + 1) * WINDOW, :] = chosen.astype(BF16)
+        starts[e] = jnp.sum(start[e : e + 1, :]).astype(jnp.int32)
     mine = ids == expert
     own_slot = jnp.sum(jnp.where(mine, slot, 0.0), axis=0, keepdims=True)
     own_gate = jnp.sum(jnp.where(mine, table, 0.0), axis=0, keepdims=True)
@@ -60,8 +70,8 @@
     return chosen.astype(BF16)
 
 
-def pick_kernel(expert, routes, values, far, out, place, weights):
-    own = route(expert[0], routes, values, place, weights)
+def pick_kernel(expert, routes, values, far, out, place, weights, starts):
+    own = route(expert[0], routes, values, place, weights, starts)
     blank = jnp.zeros((SLOTS, 64), BF16)
     low = dot(jnp.concatenate([own, blank], axis=1), far[...].reshape(EXPERTS * SPLIT, 128), 1, 1)
     high = far[:, : FEATURES - SPLIT, :].reshape(EXPERTS * (FEATURES - SPLIT), 128)
@@ -83,13 +93,23 @@
     pieces[...] = (silu * up_proj * weights[...]).astype(BF16)
 
 
-def down_kernel(gathered, down, place, out):
+def close_kernel(starts, far, out, rows):
+    for e in range(EXPERTS):
+        piece = far[e * SLOTS : (e + 1) * SLOTS, :].astype(F32)
+        rows[pl.ds(starts[e], SLOTS), :] = piece
+    closed = rows[:FILLED, :].astype(BF16)
+    for near in range(NEAR_SIZE):
+        out[near] = closed
+
+
+def down_kernel(starts, gathered, down, place, out):
     rows = []
-    for expert in range(EXPERTS):
-        total = jnp.zeros((SLOTS, FEATURES), F32)
+    for e in range(EXPERTS):
+        first = pl.multiple_of(jnp.minimum(starts[e] // 8 * 8, FILLED - WINDOW), 8)
+        total = jnp.zeros((WINDOW, FEATURES), F32)
         for near in range(0, NEAR_SIZE, 2):
-            pair = [gathered[near, expert], gathered[near + 1, expert]]
-            low = expert * HIDDEN_SIZE + near * 128
+            pair = [gathered[near + i, pl.ds(first, WINDOW), :] for i in range(2)]
+            low = e * HIDDEN_SIZE + near * 128
             total = total + dot(jnp.concatenate(pair, axis=1), down[:, low : low + 256], 1, 1)
         rows.append(total)
     rows = jnp.concatenate(rows, axis=0)
@@ -109,12 +129,13 @@
     expert = lax.axis_index("expert_0").reshape(1)
     (packed,) = call(pack_kernel, "pack", [((SPLIT, 128), BF16)], (tokens.T,))
     far = lax.all_gather(packed[None], "expert_0", tiled=True)
-    near, place, weights = call(
+    near, place, weights, starts = call(
         pick_kernel,
         "pick",
-        [((NEAR_SIZE, SLOTS, TALL), BF16), ((EXPERTS * SLOTS, TOKENS), BF16), ((SLOTS, 1), F32)],
+        [((NEAR_SIZE, SLOTS, TALL), BF16), ((EXPERTS * WINDOW, TOKENS), BF16), ((SLOTS, 1), F32), ((EXPERTS,), jnp.int32)],
         (expert, routes.T, gate_values.T, far),
         in_specs=[SMEM, VMEM, VMEM, VMEM],
+        out_specs=[VMEM, VMEM, VMEM, SMEM],
     )
     parts = lax.all_to_all(near, NEAR, 0, 0)
     shape = (EXPERTS, NEAR_SIZE, FEATURES, 128)
@@ -124,11 +145,22 @@
         [((SLOTS, 128), BF16)],
         (parts, gate_weight.reshape(shape), up_weight.reshape(shape), weights),
     )
-    far = lax.all_gather(pieces[None], "expert_0", tiled=True)
-    near = jnp.broadcast_to(far[None], (NEAR_SIZE, *far.shape))
+    far = lax.all_gather(pieces, "expert_0", tiled=True)
+    (near,) = call(
+        close_kernel,
+        "close",
+        [((NEAR_SIZE, FILLED, 128), BF16)],
+        (starts, far),
+        in_specs=[SMEM, VMEM],
+        scratch_shapes=[pltpu.VMEM((FILLED + SLOTS, 128), F32)],
+    )
     gathered = lax.all_to_all(near, NEAR, 0, 0)
     (out,) = call(
-        down_kernel, "down", [((FEATURES, TOKENS), BF16)], (gathered, down_weight.T, place)
+        down_kernel,
+        "down",
+        [((FEATURES, TOKENS), BF16)],
+        (starts, gathered, down_weight.T, place),
+        in_specs=[SMEM, VMEM, VMEM, VMEM],
     )
     return out.T
 

time: 113 us -> 113 us (level)
  blocking collectives: 110 us -> 108 us
  Pallas kernels: 2.61 us -> 4.36 us
    pallas_call x4 -> x5, Pallas kernels: 2.61 us -> 4.36 us  [call(): pl.pallas_call(kernel, out_shape=out, compiler_params=LIMIT, cost_estimat...]
    all_to_all x1, blocking collectives: 15.4 us -> 14 us  [body(): gathered = lax.all_to_all(near, NEAR, 0, 0)]
where the time goes in v5:
time: 113 us
  blocking collectives  108 us (96%)
  Pallas kernels  4.36 us (4%)
    all_gather x1, blocking collectives, body(): far = lax.all_gather(packed[None], 'expert_0', tiled=True)  47.5 us
    all_gather x1, blocking collectives, body(): far = lax.all_gather(pieces, 'expert_0', tiled=True)  32.5 us
    all_to_all x1, blocking collectives, body(): parts = lax.all_to_all(near, NEAR, 0, 0)  14.1 us
    all_to_all x1, blocking collectives, body(): gathered = lax.all_to_all(near, NEAR, 0, 0)  14 us
    pallas_call x5, Pallas kernels, call(): pl.pallas_call(kernel, out_shape=out, compiler_params=LIMIT, cost_estimat...  4.36 us

profile of v5, /device:TPU:6, one launch (start us, length us, event | category | flops | bytes accessed | tf_op | source)
XLA Modules:
  0.0 113.2 jit_solution(1789669917872694058)
XLA Ops:
  0.0 0.0 copy-start.3
  0.0 0.7 copy-done.3
  0.7 0.0 copy-start.4
  0.7 0.0 copy-start.5
  0.7 0.1 pack.1
  0.8 47.5 %all-gather = bf16[512,128]{1,0:T(8,128)(2,1)S(1)} all-gather(bf16[32,128]{1,0:T(8,128)(2,1)S(1)} %pack.1), channel_id=2, replica_groups=mesh['dp'=8,'expert_0'=16,'expert_1'=2,'expert_2'=4] {'expert_0'}, dimensions={0}, use_global_device_ids=true | all-gather | bytes 139264 | tf_op jit(solution)/shard_map/all_gather | solution.py:131
  48.3 0.0 copy-done.4
  48.3 0.0 copy-done.5
  48.3 0.0 copy-start
  48.3 0.0 copy-start.1
  48.3 0.9 pick.1
  49.2 14.1 %all_to_all.10.parts = bf16[8,40,896]{2,1,0:T(8,128)(2,1)S(1)} all-to-all(bf16[8,40,896]{2,1,0:T(8,128)(2,1)S(1)} %get-tuple-element.10), channel_id=1, replica_groups=mesh['dp'=8,'expert_0'=16,'expert_1'=2,'expert_2'=4] {'expert_1','expert..., dimensions={0} | all-to-all | bytes 1146880 | tf_op jit(solution)/shard_map/all_to_all | solution.py:140
  63.3 0.0 copy-done
  63.3 0.0 copy-done.1
  63.3 0.7 gates.1
  64.0 32.5 %all_gather.7.far = bf16[640,128]{1,0:T(8,128)(2,1)S(1)} all-gather(bf16[40,128]{1,0:T(8,128)(2,1)S(1)} %gates.1), channel_id=1, replica_groups=mesh['dp'=8,'expert_0'=16,'expert_1'=2,'expert_2'=4] {'expert_0'}, dimensions={0}, use_global_device_ids=true | all-gather | bytes 174080 | tf_op jit(solution)/shard_map/all_gather | solution.py:148
  96.4 0.6 close.1
  97.1 0.0 copy-start.2
  97.1 14.0 %all_to_all.11.gathered = bf16[8,512,128]{2,1,0:T(8,128)(2,1)S(1)} all-to-all(bf16[8,512,128]{2,1,0:T(8,128)(2,1)S(1)} %close.1), channel_id=1, replica_groups=mesh['dp'=8,'expert_0'=16,'expert_1'=2,'expert_2'=4] {'expert_1','expert..., dimensions={0} | all-to-all | bytes 2097152 | tf_op jit(solution)/shard_map/all_to_all | solution.py:157
  111.1 0.0 copy-done.2
  111.1 2.1 %down.1 = bf16[56,64]{1,0:T(8,128)(2,1)} custom-call(s32[16]{0:T(128)S(1)} %get-tuple-element.9.starts, bf16[8,512,128]{2,1,0:T(8,128)(2,1)S(1)} %all_to_all.11.gathered, bf16[56,16384]{1,0:T(8,128)(2,1)S(1)} %bitcast.12, bf16[768,64]{1,0:T(8,128)(2,1)S(1)} %get-tuple-element.12.place), custom_call_target="tpu_custom_call" | custom-call | flops 10000000000 | bytes 60000000 | tf_op jit(solution)/shard_map/down/pallas_call | solution.py:123
Async XLA Ops:
  0.0 0.7 copy-start.3
  0.7 47.5 %copy-start.4 = (s32[64,8]{0,1:T(8,128)S(1)}, s32[64,8]{0,1:T(8,128)}, u32[]{:S(2)}) copy-start(s32[64,8]{0,1:T(8,128)} %param.7) | copy-start | bytes 6148
  0.7 47.6 %copy-start.5 = (bf16[64,8]{0,1:T(8,128)(2,1)S(1)}, bf16[64,8]{0,1:T(8,128)(2,1)}, u32[]{:S(2)}) copy-start(bf16[64,8]{0,1:T(8,128)(2,1)} %param.8) | copy-start | bytes 3076
  48.3 15.0 %copy-start = (bf16[7168,128]{1,0:T(8,128)(2,1)S(1)}, bf16[7168,128]{1,0:T(8,128)(2,1)}, u32[]{:S(2)}) copy-start(bf16[7168,128]{1,0:T(8,128)(2,1)} %param.9) | copy-start | bytes 5505028
  48.3 15.0 %copy-start.1 = (bf16[7168,128]{1,0:T(8,128)(2,1)S(1)}, bf16[7168,128]{1,0:T(8,128)(2,1)}, u32[]{:S(2)}) copy-start(bf16[7168,128]{1,0:T(8,128)(2,1)} %param.10) | copy-start | bytes 5505028
  97.1 14.0 %copy-start.2 = (bf16[16384,56]{0,1:T(8,128)(2,1)S(1)}, bf16[16384,56]{0,1:T(8,128)(2,1)}, u32[]{:S(2)}) copy-start(bf16[16384,56]{0,1:T(8,128)(2,1)} %param.11) | copy-start | bytes 5505028

commit v6 on v5

--- a/solution.py
+++ b/solution.py
@@ -61,7 +61,8 @@
     for e in range(EXPERTS):
         chosen = jnp.where(shifted[e : e + 1, :] == rows, 1.0, 0.0)
         place[e * WINDOW : (e + 1) * WINDOW, :] = chosen.astype(BF16)
-        starts[e] = jnp.sum(start[e : e + 1, :]).astype(jnp.int32)
+    counts = dot(jnp.ones((8, TOKENS), BF16), present.astype(BF16), 1, 1).astype(BF16)
+    starts[...] = dot(counts, jnp.where(before, 1.0, 0.0).astype(BF16), 1, 1)[:1].astype(jnp.int32)
     mine = ids == expert
     own_slot = jnp.sum(jnp.where(mine, slot, 0.0), axis=0, keepdims=True)
     own_gate = jnp.sum(jnp.where(mine, table, 0.0), axis=0, keepdims=True)
@@ -96,7 +97,7 @@
 def close_kernel(starts, far, out, rows):
     for e in range(EXPERTS):
         piece = far[e * SLOTS : (e + 1) * SLOTS, :].astype(F32)
-        rows[pl.ds(starts[e], SLOTS), :] = piece
+        rows[pl.ds(starts[0, e], SLOTS), :] = piece
     closed = rows[:FILLED, :].astype(BF16)
     for near in range(NEAR_SIZE):
         out[near] = closed
@@ -105,7 +106,7 @@
 def down_kernel(starts, gathered, down, place, out):
     rows = []
     for e in range(EXPERTS):
-        first = pl.multiple_of(jnp.minimum(starts[e] // 8 * 8, FILLED - WINDOW), 8)
+        first = pl.multiple_of(jnp.minimum(starts[0, e] // 8 * 8, FILLED - WINDOW), 8)
         total = jnp.zeros((WINDOW, FEATURES), F32)
         for near in range(0, NEAR_SIZE, 2):
             pair = [gathered[near + i, pl.ds(first, WINDOW), :] for i in range(2)]
@@ -132,10 +133,9 @@
     near, place, weights, starts = call(
         pick_kernel,
         "pick",
-        [((NEAR_SIZE, SLOTS, TALL), BF16), ((EXPERTS * WINDOW, TOKENS), BF16), ((SLOTS, 1), F32), ((EXPERTS,), jnp.int32)],
+        [((NEAR_SIZE, SLOTS, TALL), BF16), ((EXPERTS * WINDOW, TOKENS), BF16), ((SLOTS, 1), F32), ((1, EXPERTS), jnp.int32)],
         (expert, routes.T, gate_values.T, far),
         in_specs=[SMEM, VMEM, VMEM, VMEM],
-        out_specs=[VMEM, VMEM, VMEM, SMEM],
     )
     parts = lax.all_to_all(near, NEAR, 0, 0)
     shape = (EXPERTS, NEAR_SIZE, FEATURES, 128)

time: 113 us -> 113 us (level)
  no operation moved by 1% of the time
where the time goes in v6:
time: 113 us
  blocking collectives  108 us (96%)
  Pallas kernels  3.8 us (3%)
    all_gather x1, blocking collectives, body(): far = lax.all_gather(packed[None], 'expert_0', tiled=True)  47.5 us
    all_gather x1, blocking collectives, body(): far = lax.all_gather(pieces, 'expert_0', tiled=True)  32.4 us
    all_to_all x1, blocking collectives, body(): parts = lax.all_to_all(near, NEAR, 0, 0)  14.1 us
    all_to_all x1, blocking collectives, body(): gathered = lax.all_to_all(near, NEAR, 0, 0)  14 us
    pallas_call x5, Pallas kernels, call(): pl.pallas_call(kernel, out_shape=out, compiler_params=LIMIT, cost_estimat...  3.8 us

profile of v6, /device:TPU:6, one launch (start us, length us, event | category | flops | bytes accessed | tf_op | source)
XLA Modules:
  0.0 112.5 jit_solution(12017055776600964504)
XLA Ops:
  0.0 0.0 copy-start.3
  0.0 0.7 copy-done.3
  0.7 0.0 copy-start.4
  0.7 0.0 copy-start.5
  0.7 0.1 pack.1
  0.8 47.5 %all-gather = bf16[512,128]{1,0:T(8,128)(2,1)S(1)} all-gather(bf16[32,128]{1,0:T(8,128)(2,1)S(1)} %pack.1), channel_id=2, replica_groups=mesh['dp'=8,'expert_0'=16,'expert_1'=2,'expert_2'=4] {'expert_0'}, dimensions={0}, use_global_device_ids=true | all-gather | bytes 139264 | tf_op jit(solution)/shard_map/all_gather | solution.py:132
  48.3 0.0 copy-done.4
  48.3 0.0 copy-done.5
  48.3 0.0 copy-start
  48.3 0.0 copy-start.1
  48.3 0.3 pick.1
  48.6 14.1 %all_to_all.10.parts = bf16[8,40,896]{2,1,0:T(8,128)(2,1)S(1)} all-to-all(bf16[8,40,896]{2,1,0:T(8,128)(2,1)S(1)} %get-tuple-element.10), channel_id=1, replica_groups=mesh['dp'=8,'expert_0'=16,'expert_1'=2,'expert_2'=4] {'expert_1','expert..., dimensions={0} | all-to-all | bytes 1146880 | tf_op jit(solution)/shard_map/all_to_all | solution.py:140
  62.7 0.0 copy-done
  62.7 0.0 copy-done.1
  62.7 0.7 gates.1
  63.4 32.4 %all_gather.7.far = bf16[640,128]{1,0:T(8,128)(2,1)S(1)} all-gather(bf16[40,128]{1,0:T(8,128)(2,1)S(1)} %gates.1), channel_id=1, replica_groups=mesh['dp'=8,'expert_0'=16,'expert_1'=2,'expert_2'=4] {'expert_0'}, dimensions={0}, use_global_device_ids=true | all-gather | bytes 174080 | tf_op jit(solution)/shard_map/all_gather | solution.py:148
  95.8 0.6 close.1
  96.5 0.0 copy-start.2
  96.5 14.0 %all_to_all.11.gathered = bf16[8,512,128]{2,1,0:T(8,128)(2,1)S(1)} all-to-all(bf16[8,512,128]{2,1,0:T(8,128)(2,1)S(1)} %close.1), channel_id=1, replica_groups=mesh['dp'=8,'expert_0'=16,'expert_1'=2,'expert_2'=4] {'expert_1','expert..., dimensions={0} | all-to-all | bytes 2097152 | tf_op jit(solution)/shard_map/all_to_all | solution.py:157
  110.5 0.0 copy-done.2
  110.5 2.1 %down.1 = bf16[56,64]{1,0:T(8,128)(2,1)} custom-call(s32[1,16]{1,0:T(1,128)S(1)} %get-tuple-element.9.starts, bf16[8,512,128]{2,1,0:T(8,128)(2,1)S(1)} %all_to_all.11.gathered, bf16[56,16384]{1,0:T(8,128)(2,1)S(1)} %bitcast.12, bf16[768,64]{1,0:T(8,128)(2,1)S(1)} %get-tuple-element.12.place), custom_call_target="tpu_custom_call" | custom-call | flops 10000000000 | bytes 60000000 | tf_op jit(solution)/shard_map/down/pallas_call | solution.py:124
Async XLA Ops:
  0.0 0.7 copy-start.3
  0.7 47.5 %copy-start.4 = (s32[64,8]{0,1:T(8,128)S(1)}, s32[64,8]{0,1:T(8,128)}, u32[]{:S(2)}) copy-start(s32[64,8]{0,1:T(8,128)} %param.7) | copy-start | bytes 6148
  0.7 47.6 %copy-start.5 = (bf16[64,8]{0,1:T(8,128)(2,1)S(1)}, bf16[64,8]{0,1:T(8,128)(2,1)}, u32[]{:S(2)}) copy-start(bf16[64,8]{0,1:T(8,128)(2,1)} %param.8) | copy-start | bytes 3076
  48.3 14.5 %copy-start = (bf16[7168,128]{1,0:T(8,128)(2,1)S(1)}, bf16[7168,128]{1,0:T(8,128)(2,1)}, u32[]{:S(2)}) copy-start(bf16[7168,128]{1,0:T(8,128)(2,1)} %param.9) | copy-start | bytes 5505028
  48.3 14.5 %copy-start.1 = (bf16[7168,128]{1,0:T(8,128)(2,1)S(1)}, bf16[7168,128]{1,0:T(8,128)(2,1)}, u32[]{:S(2)}) copy-start(bf16[7168,128]{1,0:T(8,128)(2,1)} %param.10) | copy-start | bytes 5505028
  96.5 14.0 %copy-start.2 = (bf16[16384,56]{0,1:T(8,128)(2,1)S(1)}, bf16[16384,56]{0,1:T(8,128)(2,1)}, u32[]{:S(2)}) copy-start(bf16[16384,56]{0,1:T(8,128)(2,1)} %param.11) | copy-start | bytes 5505028

commit v7 on v6

--- a/solution.py
+++ b/solution.py
@@ -62,7 +62,9 @@
         chosen = jnp.where(shifted[e : e + 1, :] == rows, 1.0, 0.0)
         place[e * WINDOW : (e + 1) * WINDOW, :] = chosen.astype(BF16)
     counts = dot(jnp.ones((8, TOKENS), BF16), present.astype(BF16), 1, 1).astype(BF16)
-    starts[...] = dot(counts, jnp.where(before, 1.0, 0.0).astype(BF16), 1, 1)[:1].astype(jnp.int32)
+    row = dot(counts, jnp.where(before, 1.0, 0.0).astype(BF16), 1, 1)[:1]
+    starts[:1] = row.astype(jnp.int32)
+    starts[1:] = jnp.minimum(jnp.floor(row * 0.125) * 8.0, float(FILLED - WINDOW)).astype(jnp.int32)
     mine = ids == expert
     own_slot = jnp.sum(jnp.where(mine, slot, 0.0), axis=0, keepdims=True)
     own_gate = jnp.sum(jnp.where(mine, table, 0.0), axis=0, keepdims=True)
@@ -106,13 +108,10 @@
 def down_kernel(starts, gathered, down, place, out):
     rows = []
     for e in range(EXPERTS):
-        first = pl.multiple_of(jnp.minimum(starts[0, e] // 8 * 8, FILLED - WINDOW), 8)
-        total = jnp.zeros((WINDOW, FEATURES), F32)
-        for near in range(0, NEAR_SIZE, 2):
-            pair = [gathered[near + i, pl.ds(first, WINDOW), :] for i in range(2)]
-            low = e * HIDDEN_SIZE + near * 128
-            total = total + dot(jnp.concatenate(pair, axis=1), down[:, low : low + 256], 1, 1)
-        rows.append(total)
+        first = pl.multiple_of(starts[1, e], 8)
+        near = [gathered[i, pl.ds(first, WINDOW), :] for i in range(NEAR_SIZE)]
+        low = e * HIDDEN_SIZE
+        rows.append(dot(jnp.concatenate(near, axis=1), down[:, low : low + HIDDEN_SIZE], 1, 1))
     rows = jnp.concatenate(rows, axis=0)
     coarse = rows.astype(BF16)
     fine = (rows - coarse.astype(F32)).astype(BF16)
@@ -133,7 +132,7 @@
     near, place, weights, starts = call(
         pick_kernel,
         "pick",
-        [((NEAR_SIZE, SLOTS, TALL), BF16), ((EXPERTS * WINDOW, TOKENS), BF16), ((SLOTS, 1), F32), ((1, EXPERTS), jnp.int32)],
+        [((NEAR_SIZE, SLOTS, TALL), BF16), ((EXPERTS * WINDOW, TOKENS), BF16), ((SLOTS, 1), F32), ((2, EXPERTS), jnp.int32)],
         (expert, routes.T, gate_values.T, far),
         in_specs=[SMEM, VMEM, VMEM, VMEM],
     )

time: 113 us -> 113 us (level)
  no operation moved by 1% of the time
where the time goes in v7:
time: 113 us
  blocking collectives  108 us (96%)
  Pallas kernels  3.82 us (3%)
    all_gather x1, blocking collectives, body(): far = lax.all_gather(packed[None], 'expert_0', tiled=True)  47.5 us
    all_gather x1, blocking collectives, body(): far = lax.all_gather(pieces, 'expert_0', tiled=True)  32.4 us
    all_to_all x1, blocking collectives, body(): parts = lax.all_to_all(near, NEAR, 0, 0)  14.1 us
    all_to_all x1, blocking collectives, body(): gathered = lax.all_to_all(near, NEAR, 0, 0)  14 us
    pallas_call x5, Pallas kernels, call(): pl.pallas_call(kernel, out_shape=out, compiler_params=LIMIT, cost_estimat...  3.82 us

profile of v7, /device:TPU:6, one launch (start us, length us, event | category | flops | bytes accessed | tf_op | source)
XLA Modules:
  0.0 112.6 jit_solution(3522760545132097190)
XLA Ops:
  0.0 0.0 copy-start.3
  0.0 0.7 copy-done.3
  0.7 0.0 copy-start.4
  0.7 0.0 copy-start.5
  0.7 0.1 pack.1
  0.8 47.5 %all-gather = bf16[512,128]{1,0:T(8,128)(2,1)S(1)} all-gather(bf16[32,128]{1,0:T(8,128)(2,1)S(1)} %pack.1), channel_id=2, replica_groups=mesh['dp'=8,'expert_0'=16,'expert_1'=2,'expert_2'=4] {'expert_0'}, dimensions={0}, use_global_device_ids=true | all-gather | bytes 139264 | tf_op jit(solution)/shard_map/all_gather | solution.py:131
  48.3 0.0 copy-done.4
  48.3 0.0 copy-done.5
  48.3 0.0 copy-start
  48.3 0.0 copy-start.1
  48.3 0.3 pick.1
  48.6 14.1 %all_to_all.10.parts = bf16[8,40,896]{2,1,0:T(8,128)(2,1)S(1)} all-to-all(bf16[8,40,896]{2,1,0:T(8,128)(2,1)S(1)} %get-tuple-element.10), channel_id=1, replica_groups=mesh['dp'=8,'expert_0'=16,'expert_1'=2,'expert_2'=4] {'expert_1','expert..., dimensions={0} | all-to-all | bytes 1146880 | tf_op jit(solution)/shard_map/all_to_all | solution.py:139
  62.7 0.0 copy-done
  62.7 0.0 copy-done.1
  62.7 0.7 gates.1
  63.4 32.4 %all_gather.7.far = bf16[640,128]{1,0:T(8,128)(2,1)S(1)} all-gather(bf16[40,128]{1,0:T(8,128)(2,1)S(1)} %gates.1), channel_id=1, replica_groups=mesh['dp'=8,'expert_0'=16,'expert_1'=2,'expert_2'=4] {'expert_0'}, dimensions={0}, use_global_device_ids=true | all-gather | bytes 174080 | tf_op jit(solution)/shard_map/all_gather | solution.py:147
  95.8 0.6 close.1
  96.5 0.0 copy-start.2
  96.5 14.0 %all_to_all.11.gathered = bf16[8,512,128]{2,1,0:T(8,128)(2,1)S(1)} all-to-all(bf16[8,512,128]{2,1,0:T(8,128)(2,1)S(1)} %close.1), channel_id=1, replica_groups=mesh['dp'=8,'expert_0'=16,'expert_1'=2,'expert_2'=4] {'expert_1','expert..., dimensions={0} | all-to-all | bytes 2097152 | tf_op jit(solution)/shard_map/all_to_all | solution.py:156
  110.5 0.0 copy-done.2
  110.5 2.1 %down.1 = bf16[56,64]{1,0:T(8,128)(2,1)} custom-call(s32[2,16]{1,0:T(2,128)S(1)} %get-tuple-element.9.starts, bf16[8,512,128]{2,1,0:T(8,128)(2,1)S(1)} %all_to_all.11.gathered, bf16[56,16384]{1,0:T(8,128)(2,1)S(1)} %bitcast.12, bf16[768,64]{1,0:T(8,128)(2,1)S(1)} %get-tuple-element.12.place), custom_call_target="tpu_custom_call" | custom-call | flops 10000000000 | bytes 60000000 | tf_op jit(solution)/shard_map/down/pallas_call | solution.py:123
Async XLA Ops:
  0.0 0.7 copy-start.3
  0.7 47.5 %copy-start.4 = (s32[64,8]{0,1:T(8,128)S(1)}, s32[64,8]{0,1:T(8,128)}, u32[]{:S(2)}) copy-start(s32[64,8]{0,1:T(8,128)} %param.7) | copy-start | bytes 6148
  0.7 47.6 %copy-start.5 = (bf16[64,8]{0,1:T(8,128)(2,1)S(1)}, bf16[64,8]{0,1:T(8,128)(2,1)}, u32[]{:S(2)}) copy-start(bf16[64,8]{0,1:T(8,128)(2,1)} %param.8) | copy-start | bytes 3076
  48.3 14.5 %copy-start = (bf16[7168,128]{1,0:T(8,128)(2,1)S(1)}, bf16[7168,128]{1,0:T(8,128)(2,1)}, u32[]{:S(2)}) copy-start(bf16[7168,128]{1,0:T(8,128)(2,1)} %param.9) | copy-start | bytes 5505028
  48.3 14.5 %copy-start.1 = (bf16[7168,128]{1,0:T(8,128)(2,1)S(1)}, bf16[7168,128]{1,0:T(8,128)(2,1)}, u32[]{:S(2)}) copy-start(bf16[7168,128]{1,0:T(8,128)(2,1)} %param.10) | copy-start | bytes 5505028
  96.5 14.0 %copy-start.2 = (bf16[16384,56]{0,1:T(8,128)(2,1)S(1)}, bf16[16384,56]{0,1:T(8,128)(2,1)}, u32[]{:S(2)}) copy-start(bf16[16384,56]{0,1:T(8,128)(2,1)} %param.11) | copy-start | bytes 5505028
